TPU v7x, 32 devices: a whole 2x2x4 slice. The times are simulated.
32 devices in a mesh: grid: 8 (over z, y), band: 4 (over x, core).
Axes of the slice: x: 2, y: 2, z: 4, core: 2. Of those that a mesh axis runs over, the one named last changes fastest.
Arguments:
- orbitals: float32 [32, 16, 16, 512], P('grid', None, None, 'band'), may hold values from -80 to 80
- projectors: float32 [32, 16, 16, 512], P('grid', None, None, 'band'), may hold values from -0.09375 to 0.09375
- potential: float32 [32, 16, 16], P('grid'), may hold values from 0.3 to 3
Outputs:
- updated_orbitals: float32 [32, 16, 16, 512], P('grid', None, None, 'band')
- rayleigh_quotients: float32 [3, 512], P(None, 'band')
- residual_norms: float32 [3, 512], P(None, 'band')
All inputs are finite; a program needn't handle non-finite values.
Results may differ from a plain program's by a relative error of at most 0.00012.
Values sent between devices are 32-bit elements; how exact they have to be, the bound alone decides.
A program may use at most 128 MiB of HBM per device.

v0:
```python
import jax
import jax.numpy as jnp
from jax import lax
from jax.sharding import PartitionSpec as P

ITERS = 3
STENCIL = (-205.0 / 72.0, 8.0 / 5.0, -1.0 / 5.0, 8.0 / 315.0, -1.0 / 560.0)
STEP_LENGTH = 0.25
NORM_EPS = 1e-06
HIGHEST = lax.Precision.HIGHEST


def with_halo(block, sides, width):
    for axis, dim in sides:
        count = lax.axis_size(axis)
        forward = [(i, i + 1) for i in range(count - 1)]
        forward.append((count - 1, 0))
        backward = [(target, source) for source, target in forward]
        low = lax.ppermute(
            lax.slice_in_dim(block, block.shape[dim] - width, None, axis=dim), axis, forward
        )
        high = lax.ppermute(lax.slice_in_dim(block, 0, width, axis=dim), axis, backward)
        block = jnp.concatenate([low, block, high], axis=dim)
    return block


def matmul(left, right):
    return jnp.dot(left, right, precision=HIGHEST, preferred_element_type=jnp.float32)


def laplacian(grid_field):
    padded = with_halo(grid_field, (("grid", 0),), 4)
    planes_here = grid_field.shape[0]
    result = 3.0 * STENCIL[0] * grid_field
    for distance in range(1, 5):
        result = result + STENCIL[distance] * (
            padded[4 + distance : 4 + distance + planes_here]
            + padded[4 - distance : 4 - distance + planes_here]
        )
    for dimension in (1, 2):
        for distance in range(1, 5):
            result = result + STENCIL[distance] * (
                jnp.roll(grid_field, distance, dimension)
                + jnp.roll(grid_field, -distance, dimension)
            )
    return result


def local(orbitals, projectors, potential):
    grid_shape = orbitals.shape
    local_bands = orbitals.shape[3]
    total_bands = local_bands * lax.axis_size("band")
    first_band = lax.axis_index("band") * local_bands
    vectors = orbitals.reshape(-1, local_bands)
    every_projector = lax.all_gather(projectors, "band", axis=3, tiled=True).reshape(
        -1, projectors.shape[3] * lax.axis_size("band")
    )
    identity_matrix = jnp.eye(total_bands, dtype=jnp.float32)
    quotient_list = []
    norm_list = []
    for iteration in range(ITERS):
        gathered = lax.all_gather(vectors.reshape(grid_shape), "band", axis=3, tiled=True).reshape(
            -1, total_bands
        )
        margin = lax.psum(matmul(gathered.T, gathered), "grid")
        factor = jnp.linalg.cholesky(margin)
        inverse = jax.scipy.linalg.solve_triangular(factor, identity_matrix, lower=True)
        transform = inverse.T
        vectors = matmul(gathered, lax.dynamic_slice_in_dim(transform, first_band, local_bands, 1))
        coupling = lax.psum(matmul(every_projector.T, vectors), "grid")
        exchange_part = matmul(every_projector, coupling)
        grid_field = vectors.reshape(grid_shape)
        applied = (-0.5 * laplacian(grid_field) + potential[..., None] * grid_field).reshape(
            -1, local_bands
        ) - exchange_part
        rayleigh = lax.psum(jnp.sum(vectors * applied, axis=0), "grid")
        residual = applied - rayleigh[None, :] * vectors
        squared = lax.psum(jnp.sum(residual * residual, axis=0), "grid")
        vectors = vectors - STEP_LENGTH * residual / jnp.sqrt(squared + NORM_EPS)[None, :]
        quotient_list.append(rayleigh)
        norm_list.append(jnp.sqrt(squared))
    return (vectors.reshape(grid_shape), jnp.stack(quotient_list), jnp.stack(norm_list))


def solution(mesh):
    return jax.shard_map(
        local,
        mesh=mesh,
        in_specs=(
            P("grid", None, None, "band"),
            P("grid", None, None, "band"),
            P("grid", None, None),
        ),
        out_specs=(P("grid", None, None, "band"), P(None, "band"), P(None, "band")),
        check_vma=False,
    )
```

profile of v0, /device:TPU:0, one launch (start us, length us, event | category | flops | bytes accessed | tf_op | source)
XLA Modules:
  0.0 1202.1 jit_solution(3516485684897773808)
XLA Ops:
  7.9 27.1 %all-gather.5.cloned.1.call-done = f32[4,16,16,512]{3,2,1,0:T(8,128)} async-done(((f32[4,16,16,128]{3,2,1,0:T(8,128)}), f32[4,16,16,512]{3,2,1,0:T(8,128)}) %all-gather.5.cloned.1.call-update) | async-done | bytes 2097168 | tf_op jit(solution)/shard_map/all_gather | solution.py:62
  35.1 6.7 convolution_bitcast_fusion.2
  43.0 77.3 %all-reduce.8.cloned.1.call-done = f32[512,512]{0,1:T(8,128)} async-done(((f32[512,512]{0,1:T(8,128)}), f32[512,512]{0,1:T(8,128)}) %all-reduce.8.cloned.1.call-update) | async-done | bytes 1048592 | tf_op jit(solution)/shard_map/psum | solution.py:65
  123.2 11.7 cholesky.374
  134.9 9.8 custom-call.31
  147.4 11.7 cholesky.393
  159.2 10.3 custom-call.32
  171.0 11.7 cholesky.414
  183.5 9.8 custom-call.33
  194.7 11.7 cholesky.431
  210.6 8.1 while.6
  218.7 39.3 %custom-call.34 = f32[4,128,128]{1,2,0:T(8,128)S(1)} custom-call(f32[4,128,128]{2,1,0:T(8,128)S(1)} %get-tuple-element.25), custom_call_target="InvertDiagBlocksLowerTriangular" | custom-call | tf_op jit(solution)/shard_map/jit(_solve_triangular)/triangular_solve | solution.py:67
  282.4 6.2 collective-permute-done
  296.4 58.0 %all-reduce.10.cloned.1.call-done = f32[512,128]{0,1:T(8,128)} async-done(((f32[512,128]{0,1:T(8,128)}), f32[512,128]{0,1:T(8,128)}) %all-reduce.10.cloned.1.call-update) | async-done | bytes 262160 | tf_op jit(solution)/shard_map/psum | solution.py:70
  357.9 19.6 %psum.86 = f32[128]{0:T(128)S(1)} all-reduce(f32[128]{0:T(128)S(1)} %get-tuple-element.195), channel_id=1, replica_groups=mesh['grid'=8,'band'=4] {'grid'}, use_global_device_ids=true, to_apply=%region_11.14 | all-reduce | flops 128 | bytes 1024 | tf_op jit(solution)/shard_map/psum | solution.py:76
  377.8 17.1 %psum.87 = f32[128]{0:T(128)S(1)} all-reduce(f32[128]{0:T(128)S(1)} %multiply_reduce_fusion.4), channel_id=1, replica_groups=mesh['grid'=8,'band'=4] {'grid'}, use_global_device_ids=true, to_apply=%region_13.16 | all-reduce | flops 128 | bytes 1024 | tf_op jit(solution)/shard_map/psum | solution.py:78
  398.0 21.6 %all-gather.9.cloned.1.call-done = f32[4,16,16,512]{3,2,1,0:T(8,128)} async-done(((f32[4,16,16,128]{3,2,1,0:T(8,128)}), f32[4,16,16,512]{3,2,1,0:T(8,128)}) %all-gather.9.cloned.1.call-update) | async-done | bytes 2097168 | tf_op jit(solution)/shard_map/all_gather | solution.py:62
  419.6 6.7 convolution_bitcast_fusion.1
  426.8 77.9 %all-reduce.12.cloned.1.call-done = f32[512,512]{0,1:T(8,128)} async-done(((f32[512,512]{0,1:T(8,128)}), f32[512,512]{0,1:T(8,128)}) %all-reduce.12.cloned.1.call-update) | async-done | bytes 1048592 | tf_op jit(solution)/shard_map/psum | solution.py:65
  509.8 11.7 cholesky.446
  521.7 9.8 custom-call.35
  534.0 11.7 cholesky.465
  547.1 9.9 custom-call.36
  559.6 11.7 cholesky.486
  572.6 9.8 custom-call.37
  584.6 11.7 cholesky.503
  602.6 11.8 while.7
  615.1 40.1 %custom-call.38 = f32[4,128,128]{1,2,0:T(8,128)S(1)} custom-call(f32[4,128,128]{2,1,0:T(8,128)} %copy-done.45), custom_call_target="InvertDiagBlocksLowerTriangular" | custom-call | tf_op jit(solution)/shard_map/jit(_solve_triangular)/triangular_solve | solution.py:67
  680.7 14.4 %collective-permute-done.2 = f32[4,16,16,128]{3,2,1,0:T(8,128)} collective-permute-done((f32[4,16,16,128]{3,2,1,0:T(8,128)S(1)}, f32[4,16,16,128]{3,2,1,0:T(8,128)}, u32[]{:S(2)}, u32[]{:S(2)}) %collective-permute-start.2) | collective-permute-done | bytes 524320 | tf_op jit(solution)/shard_map/ppermute | solution.py:22
  701.9 51.0 %all-reduce.14.cloned.1.call-done = f32[512,128]{0,1:T(8,128)} async-done(((f32[512,128]{0,1:T(8,128)}), f32[512,128]{0,1:T(8,128)}) %all-reduce.14.cloned.1.call-update) | async-done | bytes 262160 | tf_op jit(solution)/shard_map/psum | solution.py:70
  756.4 19.6 %psum.90 = f32[128]{0:T(128)S(1)} all-reduce(f32[128]{0:T(128)S(1)} %get-tuple-element.199), channel_id=1, replica_groups=mesh['grid'=8,'band'=4] {'grid'}, use_global_device_ids=true, to_apply=%region_17.20 | all-reduce | flops 128 | bytes 1024 | tf_op jit(solution)/shard_map/psum | solution.py:76
  776.2 17.1 %psum.91 = f32[128]{0:T(128)S(1)} all-reduce(f32[128]{0:T(128)S(1)} %multiply_reduce_fusion.2), channel_id=1, replica_groups=mesh['grid'=8,'band'=4] {'grid'}, use_global_device_ids=true, to_apply=%region_19.22 | all-reduce | flops 128 | bytes 1024 | tf_op jit(solution)/shard_map/psum | solution.py:78
  797.0 21.6 %all-gather.11.cloned.1.call-done = f32[4,16,16,512]{3,2,1,0:T(8,128)} async-done(((f32[4,16,16,128]{3,2,1,0:T(8,128)}), f32[4,16,16,512]{3,2,1,0:T(8,128)}) %all-gather.11.cloned.1.call-update) | async-done | bytes 2097168 | tf_op jit(solution)/shard_map/all_gather | solution.py:62
  818.6 6.7 convolution_bitcast_fusion
  825.5 78.3 %all-reduce.16.cloned.1.call-done = f32[512,512]{0,1:T(8,128)} async-done(((f32[512,512]{0,1:T(8,128)}), f32[512,512]{0,1:T(8,128)}) %all-reduce.16.cloned.1.call-update) | async-done | bytes 1048592 | tf_op jit(solution)/shard_map/psum | solution.py:65
  908.8 11.7 cholesky.518
  920.7 9.8 custom-call.39
  933.1 11.7 cholesky.537
  946.1 10.0 custom-call.40
  958.7 11.7 cholesky.558
  971.7 9.8 custom-call.41
  983.7 11.7 cholesky.575
  1001.9 11.8 while.8
  1014.4 40.1 %custom-call.42 = f32[4,128,128]{1,2,0:T(8,128)S(1)} custom-call(f32[4,128,128]{2,1,0:T(8,128)} %copy-done.44), custom_call_target="InvertDiagBlocksLowerTriangular" | custom-call | tf_op jit(solution)/shard_map/jit(_solve_triangular)/triangular_solve | solution.py:67
  1079.6 14.8 %collective-permute-done.4 = f32[4,16,16,128]{3,2,1,0:T(8,128)} collective-permute-done((f32[4,16,16,128]{3,2,1,0:T(8,128)S(1)}, f32[4,16,16,128]{3,2,1,0:T(8,128)}, u32[]{:S(2)}, u32[]{:S(2)}) %collective-permute-start.4) | collective-permute-done | bytes 524320 | tf_op jit(solution)/shard_map/ppermute | solution.py:22
  1101.2 51.0 %all-reduce.18.cloned.1.call-done = f32[512,128]{0,1:T(8,128)} async-done(((f32[512,128]{0,1:T(8,128)}), f32[512,128]{0,1:T(8,128)}) %all-reduce.18.cloned.1.call-update) | async-done | bytes 262160 | tf_op jit(solution)/shard_map/psum | solution.py:70
  1155.7 19.6 %psum.94 = f32[128]{0:T(128)S(1)} all-reduce(f32[128]{0:T(128)S(1)} %get-tuple-element.203), channel_id=1, replica_groups=mesh['grid'=8,'band'=4] {'grid'}, use_global_device_ids=true, to_apply=%region_23.26 | all-reduce | flops 128 | bytes 1024 | tf_op jit(solution)/shard_map/psum | solution.py:76
  1175.5 17.1 %psum.95 = f32[128]{0:T(128)S(1)} all-reduce(f32[128]{0:T(128)S(1)} %multiply_reduce_fusion), channel_id=1, replica_groups=mesh['grid'=8,'band'=4] {'grid'}, use_global_device_ids=true, to_apply=%region_25.28 | all-reduce | flops 128 | bytes 1024 | tf_op jit(solution)/shard_map/psum | solution.py:78
  (329 shorter events, 200.2 us)
Async XLA Ops:
  7.2 27.9 %all-gather.5.cloned.1.call-start = ((), (), s32[]{:S(2)}) async-start(), calls=%async_computation | async-start | bytes 2621440 | tf_op jit(solution)/shard_map/all_gather | solution.py:62
  7.9 112.4 %all-reduce.8.cloned.1.call-start = ((), (), s32[]{:S(2)}) async-start(), calls=%async_computation.1 | async-start | bytes 2097152 | tf_op jit(solution)/shard_map/psum | solution.py:65
  41.8 236.4 %all-gather.7.cloned.1.call-start = ((), (), s32[]{:S(2)}) async-start(), calls=%async_computation.2 | async-start | bytes 2621440 | tf_op jit(solution)/shard_map/all_gather | solution.py:55
  42.5 311.9 %all-reduce.10.cloned.1.call-start = ((), (), s32[]{:S(2)}) async-start(), calls=%async_computation.3 | async-start | bytes 524288 | tf_op jit(solution)/shard_map/psum | solution.py:70
  43.0 217.1 %copy-start.4 = (f32[512,512]{1,0:T(8,128)}, f32[512,512]{1,0:T(8,128)S(1)}, u32[]{:S(2)}) copy-start(f32[512,512]{1,0:T(8,128)S(1)} %fusion.6) | copy-start | bytes 3145732
  263.7 24.9 %collective-permute-start = (f32[4,16,16,128]{3,2,1,0:T(8,128)S(1)}, f32[4,16,16,128]{3,2,1,0:T(8,128)S(1)}, u32[]{:S(2)}, u32[]{:S(2)}) collective-permute-start(f32[4,16,16,128]{3,2,1,0:T(8,128)S(1)} %bitcast.253), channel_id=1, source_target_pairs={{4,0},{8,4},{12,8},{16,12},{20,16},{24,20},{28,24},{0,28},{5,1},{9... | collective-permute-start | bytes 1572872 | tf_op jit(solution)/shard_map/ppermute | solution.py:22
  266.7 21.9 %collective-permute-start.1 = (f32[4,16,16,128]{3,2,1,0:T(8,128)S(1)}, f32[4,16,16,128]{3,2,1,0:T(8,128)S(1)}, u32[]{:S(2)}, u32[]{:S(2)}) collective-permute-start(f32[4,16,16,128]{3,2,1,0:T(8,128)S(1)} %bitcast.254), channel_id=1, source_target_pairs={{0,4},{4,8},{8,12},{12,16},{16,20},{20,24},{24,28},{28,0},{1,5},{5... | collective-permute-start | bytes 1572872 | tf_op jit(solution)/shard_map/ppermute | solution.py:19
  281.8 137.8 %all-gather.9.cloned.1.call-start = ((), (), s32[]{:S(2)}) async-start(), calls=%async_computation.4 | async-start | bytes 2621440 | tf_op jit(solution)/shard_map/all_gather | solution.py:62
  282.1 7.5 copy-start.27
  282.1 7.5 copy-start.28
  282.1 7.5 copy-start.29
  282.1 7.4 copy-start.30
  282.1 7.4 copy-start.31
  282.2 7.4 copy-start.32
  282.2 7.4 copy-start.37
  282.2 7.4 copy-start.38
  282.2 7.4 copy-start.41
  289.6 64.8 %copy-start = (f32[4,16,16,512]{3,2,1,0:T(8,128)S(1)}, f32[4,16,16,512]{3,2,1,0:T(8,128)}, u32[]{:S(2)}) copy-start(f32[4,16,16,512]{3,2,1,0:T(8,128)} %all-gather.7.cloned.1.call-done) | copy-start | bytes 6291460
  398.0 106.8 %all-reduce.12.cloned.1.call-start = ((), (), s32[]{:S(2)}) async-start(), calls=%async_computation.5 | async-start | bytes 2097152 | tf_op jit(solution)/shard_map/psum | solution.py:65
  426.3 326.6 %all-reduce.14.cloned.1.call-start = ((), (), s32[]{:S(2)}) async-start(), calls=%async_computation.6 | async-start | bytes 524288 | tf_op jit(solution)/shard_map/psum | solution.py:70
  559.6 95.7 %copy-start.5 = (f32[512,512]{1,0:T(8,128)S(1)}, f32[512,512]{1,0:T(8,128)}, u32[]{:S(2)}) copy-start(f32[512,512]{1,0:T(8,128)} %copy-done.4) | copy-start | bytes 3145732
  669.1 26.0 %collective-permute-start.2 = (f32[4,16,16,128]{3,2,1,0:T(8,128)S(1)}, f32[4,16,16,128]{3,2,1,0:T(8,128)}, u32[]{:S(2)}, u32[]{:S(2)}) collective-permute-start(f32[4,16,16,128]{3,2,1,0:T(8,128)S(1)} %bitcast.221), channel_id=1, source_target_pairs={{4,0},{8,4},{12,8},{16,12},{20,16},{24,20},{28,24},{0,28},{5,1},{9... | collective-permute-start | bytes 1572872 | tf_op jit(solution)/shard_map/ppermute | solution.py:22
  672.0 23.1 %collective-permute-start.3 = (f32[4,16,16,128]{3,2,1,0:T(8,128)S(1)}, f32[4,16,16,128]{3,2,1,0:T(8,128)}, u32[]{:S(2)}, u32[]{:S(2)}) collective-permute-start(f32[4,16,16,128]{3,2,1,0:T(8,128)S(1)} %bitcast.222), channel_id=1, source_target_pairs={{0,4},{4,8},{8,12},{12,16},{16,20},{20,24},{24,28},{28,0},{1,5},{5... | collective-permute-start | bytes 1572872 | tf_op jit(solution)/shard_map/ppermute | solution.py:19
  680.0 138.6 %all-gather.11.cloned.1.call-start = ((), (), s32[]{:S(2)}) async-start(), calls=%async_computation.7 | async-start | bytes 2621440 | tf_op jit(solution)/shard_map/all_gather | solution.py:62
  680.4 14.7 %copy-start.15 = (f32[4,16,15,128]{3,2,1,0:T(8,128)S(1)}, f32[4,16,15,128]{3,2,1,0:T(8,128)}, u32[]{:S(2)}) copy-start(f32[4,16,15,128]{3,2,1,0:T(8,128)} %get-tuple-element.111) | copy-start | bytes 1474564
  680.5 14.7 %copy-start.16 = (f32[4,16,15,128]{3,2,1,0:T(8,128)S(1)}, f32[4,16,15,128]{3,2,1,0:T(8,128)}, u32[]{:S(2)}) copy-start(f32[4,16,15,128]{3,2,1,0:T(8,128)} %get-tuple-element.112) | copy-start | bytes 1474564
  680.5 14.7 %copy-start.17 = (f32[4,16,14,128]{3,2,1,0:T(8,128)S(1)}, f32[4,16,14,128]{3,2,1,0:T(8,128)}, u32[]{:S(2)}) copy-start(f32[4,16,14,128]{3,2,1,0:T(8,128)} %get-tuple-element.115) | copy-start | bytes 1376260
  680.5 14.7 %copy-start.18 = (f32[4,16,14,128]{3,2,1,0:T(8,128)S(1)}, f32[4,16,14,128]{3,2,1,0:T(8,128)}, u32[]{:S(2)}) copy-start(f32[4,16,14,128]{3,2,1,0:T(8,128)} %get-tuple-element.116) | copy-start | bytes 1376260
  680.5 14.7 %copy-start.19 = (f32[4,16,13,128]{3,2,1,0:T(8,128)S(1)}, f32[4,16,13,128]{3,2,1,0:T(8,128)}, u32[]{:S(2)}) copy-start(f32[4,16,13,128]{3,2,1,0:T(8,128)} %get-tuple-element.119) | copy-start | bytes 1277956
  680.5 14.7 %copy-start.20 = (f32[4,16,13,128]{3,2,1,0:T(8,128)S(1)}, f32[4,16,13,128]{3,2,1,0:T(8,128)}, u32[]{:S(2)}) copy-start(f32[4,16,13,128]{3,2,1,0:T(8,128)} %get-tuple-element.120) | copy-start | bytes 1277956
  680.5 14.7 %copy-start.33 = (f32[4,14,16,128]{3,2,1,0:T(8,128)S(1)}, f32[4,14,16,128]{3,2,1,0:T(8,128)}, u32[]{:S(2)}) copy-start(f32[4,14,16,128]{3,2,1,0:T(8,128)} %get-tuple-element.99) | copy-start | bytes 1376260
  680.5 14.7 %copy-start.34 = (f32[4,14,16,128]{3,2,1,0:T(8,128)S(1)}, f32[4,14,16,128]{3,2,1,0:T(8,128)}, u32[]{:S(2)}) copy-start(f32[4,14,16,128]{3,2,1,0:T(8,128)} %get-tuple-element.100) | copy-start | bytes 1376260
  680.5 14.7 %copy-start.42 = (f32[4,16,16]{2,1,0:T(8,128)S(1)}, f32[4,16,16]{2,1,0:T(8,128)}, u32[]{:S(2)}) copy-start(f32[4,16,16]{2,1,0:T(8,128)} %param.8) | copy-start | bytes 12292
  796.9 106.8 %all-reduce.16.cloned.1.call-start = ((), (), s32[]{:S(2)}) async-start(), calls=%async_computation.8 | async-start | bytes 2097152 | tf_op jit(solution)/shard_map/psum | solution.py:65
  825.3 326.9 %all-reduce.18.cloned.1.call-start = ((), (), s32[]{:S(2)}) async-start(), calls=%async_computation.9 | async-start | bytes 524288 | tf_op jit(solution)/shard_map/psum | solution.py:70
  958.7 95.8 %copy-start.6 = (f32[512,512]{1,0:T(8,128)S(1)}, f32[512,512]{1,0:T(8,128)}, u32[]{:S(2)}) copy-start(f32[512,512]{1,0:T(8,128)} %copy-done.4) | copy-start | bytes 3145732
  1068.4 26.0 %collective-permute-start.4 = (f32[4,16,16,128]{3,2,1,0:T(8,128)S(1)}, f32[4,16,16,128]{3,2,1,0:T(8,128)}, u32[]{:S(2)}, u32[]{:S(2)}) collective-permute-start(f32[4,16,16,128]{3,2,1,0:T(8,128)S(1)} %bitcast.240), channel_id=1, source_target_pairs={{4,0},{8,4},{12,8},{16,12},{20,16},{24,20},{28,24},{0,28},{5,1},{9... | collective-permute-start | bytes 1572872 | tf_op jit(solution)/shard_map/ppermute | solution.py:22
  1071.3 23.1 %collective-permute-start.5 = (f32[4,16,16,128]{3,2,1,0:T(8,128)S(1)}, f32[4,16,16,128]{3,2,1,0:T(8,128)}, u32[]{:S(2)}, u32[]{:S(2)}) collective-permute-start(f32[4,16,16,128]{3,2,1,0:T(8,128)S(1)} %bitcast.241), channel_id=1, source_target_pairs={{0,4},{4,8},{8,12},{12,16},{16,20},{20,24},{24,28},{28,0},{1,5},{5... | collective-permute-start | bytes 1572872 | tf_op jit(solution)/shard_map/ppermute | solution.py:19
  1079.4 15.0 %copy-start.21 = (f32[4,16,15,128]{3,2,1,0:T(8,128)S(1)}, f32[4,16,15,128]{3,2,1,0:T(8,128)}, u32[]{:S(2)}) copy-start(f32[4,16,15,128]{3,2,1,0:T(8,128)} %get-tuple-element.79) | copy-start | bytes 1474564
  1079.4 15.0 %copy-start.22 = (f32[4,16,15,128]{3,2,1,0:T(8,128)S(1)}, f32[4,16,15,128]{3,2,1,0:T(8,128)}, u32[]{:S(2)}) copy-start(f32[4,16,15,128]{3,2,1,0:T(8,128)} %get-tuple-element.80) | copy-start | bytes 1474564
  1079.4 15.0 %copy-start.23 = (f32[4,16,14,128]{3,2,1,0:T(8,128)S(1)}, f32[4,16,14,128]{3,2,1,0:T(8,128)}, u32[]{:S(2)}) copy-start(f32[4,16,14,128]{3,2,1,0:T(8,128)} %get-tuple-element.83) | copy-start | bytes 1376260
  1079.4 15.0 %copy-start.24 = (f32[4,16,14,128]{3,2,1,0:T(8,128)S(1)}, f32[4,16,14,128]{3,2,1,0:T(8,128)}, u32[]{:S(2)}) copy-start(f32[4,16,14,128]{3,2,1,0:T(8,128)} %get-tuple-element.84) | copy-start | bytes 1376260
  1079.4 15.0 %copy-start.25 = (f32[4,16,13,128]{3,2,1,0:T(8,128)S(1)}, f32[4,16,13,128]{3,2,1,0:T(8,128)}, u32[]{:S(2)}) copy-start(f32[4,16,13,128]{3,2,1,0:T(8,128)} %get-tuple-element.87) | copy-start | bytes 1277956
  1079.4 15.0 %copy-start.26 = (f32[4,16,13,128]{3,2,1,0:T(8,128)S(1)}, f32[4,16,13,128]{3,2,1,0:T(8,128)}, u32[]{:S(2)}) copy-start(f32[4,16,13,128]{3,2,1,0:T(8,128)} %get-tuple-element.88) | copy-start | bytes 1277956
  1079.4 15.0 %copy-start.35 = (f32[4,14,16,128]{3,2,1,0:T(8,128)S(1)}, f32[4,14,16,128]{3,2,1,0:T(8,128)}, u32[]{:S(2)}) copy-start(f32[4,14,16,128]{3,2,1,0:T(8,128)} %get-tuple-element.67) | copy-start | bytes 1376260
  1079.4 15.0 %copy-start.36 = (f32[4,14,16,128]{3,2,1,0:T(8,128)S(1)}, f32[4,14,16,128]{3,2,1,0:T(8,128)}, u32[]{:S(2)}) copy-start(f32[4,14,16,128]{3,2,1,0:T(8,128)} %get-tuple-element.68) | copy-start | bytes 1376260
  1079.5 15.0 %copy-start.43 = (f32[4,16,16]{2,1,0:T(8,128)S(1)}, f32[4,16,16]{2,1,0:T(8,128)}, u32[]{:S(2)}) copy-start(f32[4,16,16]{2,1,0:T(8,128)} %param.8) | copy-start | bytes 12292
  1155.7 38.2 %copy-start.46 = (f32[1,128]{1,0:T(1,128)S(1)}, f32[1,128]{1,0:T(1,128)}, u32[]{:S(2)}) copy-start(f32[1,128]{1,0:T(1,128)} %get-tuple-element.189) | copy-start | bytes 1540
  (15 other events, 26.2 us)
Sparse Core Ops, SparseCore 0:
  9.5 25.5 all-gather.4
  41.9 78.3 all-reduce.7
  121.8 22.4 all-gather.6
  282.0 72.4 all-reduce.9
  398.1 21.4 all-gather.8
  426.4 78.2 all-reduce.11
  680.1 72.7 all-reduce.13
  797.0 21.4 all-gather.10
  825.4 78.3 all-reduce.15
  1079.5 72.6 all-reduce.17
where the time goes:
time: 1210 us; the launch traced here: 1200 us
  waiting for transfers between devices  501 us (41%)
  other arithmetic  387 us (32%)
  blocking collectives  110 us (9%)
  local copies, waits for them, and re-layouts  93.1 us (8%)
  matrix products  77.4 us (6%)
  between operations  22.9 us (2%)
    another operation x44, other arithmetic, local(): factor = jnp.linalg.cholesky(margin)  240 us
    psum x3, waiting for transfers between devices, local(): margin = lax.psum(matmul(gathered.T, gathered), 'grid')  233 us
    psum x3, waiting for transfers between devices, local(): coupling = lax.psum(matmul(every_projector.T, vectors), 'grid')  160 us
    another operation x7, other arithmetic, local(): jax.scipy.linalg.solve_triangular(factor, identity_matrix, lower=True)  125 us
    all_gather x3, waiting for transfers between devices, local(): lax.all_gather(vectors.reshape(grid_shape), 'band', axis=3, tiled=True)  70.3 us
    psum x3, blocking collectives, local(): rayleigh = lax.psum(jnp.sum(vectors * applied, axis=0), 'grid')  58.9 us
    psum x3, blocking collectives, local(): squared = lax.psum(jnp.sum(residual * residual, axis=0), 'grid')  51.4 us
    dot_general x12, matrix products, matmul(): jnp.dot(left, right, precision=HIGHEST, preferred_element_type=jnp.float32)  44.3 us
  transfers between devices with their start and end apart: 16, of which 12 were waited for; matrix products, arithmetic and copies ran while one was open for 16% of the time, Pallas kernels for 0%

commit v1 on v0

--- a/solution.py
+++ b/solution.py
@@ -59,9 +59,9 @@
     quotient_list = []
     norm_list = []
     for iteration in range(ITERS):
-        gathered = lax.all_gather(vectors.reshape(grid_shape), "band", axis=3, tiled=True).reshape(
-            -1, total_bands
-        )
+        gathered = jnp.concatenate(
+            lax.all_gather(vectors.reshape(grid_shape), "band"), axis=3
+        ).reshape(-1, total_bands)
         margin = lax.psum(matmul(gathered.T, gathered), "grid")
         factor = jnp.linalg.cholesky(margin)
         inverse = jax.scipy.linalg.solve_triangular(factor, identity_matrix, lower=True)

time: 1210 us -> 1220 us (level)
  local copies, waits for them, and re-layouts: 93.1 us -> 107 us
where the time goes in v1:
time: 1220 us; the launch traced here: 1210 us
  waiting for transfers between devices  500 us (41%)
  other arithmetic  387 us (32%)
  blocking collectives  110 us (9%)
  local copies, waits for them, and re-layouts  107 us (9%)
  matrix products  70.8 us (6%)
  between operations  23.6 us (2%)
    another operation x44, other arithmetic, local(): factor = jnp.linalg.cholesky(margin)  240 us
    psum x3, waiting for transfers between devices, local(): margin = lax.psum(matmul(gathered.T, gathered), 'grid')  233 us
    psum x3, waiting for transfers between devices, local(): coupling = lax.psum(matmul(every_projector.T, vectors), 'grid')  160 us
    another operation x7, other arithmetic, local(): jax.scipy.linalg.solve_triangular(factor, identity_matrix, lower=True)  125 us
    all_gather x3, waiting for transfers between devices, local(): lax.all_gather(vectors.reshape(grid_shape), 'band')  69.6 us
    psum x3, blocking collectives, local(): rayleigh = lax.psum(jnp.sum(vectors * applied, axis=0), 'grid')  58.9 us
    psum x3, blocking collectives, local(): squared = lax.psum(jnp.sum(residual * residual, axis=0), 'grid')  51.4 us
    dot_general x12, matrix products, matmul(): jnp.dot(left, right, precision=HIGHEST, preferred_element_type=jnp.float32)  37.8 us
  transfers between devices with their start and end apart: 16, of which 12 were waited for; matrix products, arithmetic and copies ran while one was open for 16% of the time, Pallas kernels for 0%

profile of v1, /device:TPU:0, one launch (start us, length us, event | category | flops | bytes accessed | tf_op | source)
XLA Modules:
  0.0 1209.1 jit_solution(1648069849725123500)
XLA Ops:
  7.9 26.9 %all-gather.12.cloned.1.call-done = f32[16,16,16,128]{3,2,1,0:T(8,128)} async-done(((f32[4,16,16,128]{3,2,1,0:T(8,128)}), f32[16,16,16,128]{3,2,1,0:T(8,128)}) %all-gather.12.cloned.1.call-update) | async-done | bytes 2097168 | tf_op jit(solution)/shard_map/all_gather | solution.py:63
  44.9 77.2 %all-reduce.8.cloned.1.call-done = f32[512,512]{0,1:T(8,128)} async-done(((f32[512,512]{0,1:T(8,128)}), f32[512,512]{0,1:T(8,128)}) %all-reduce.8.cloned.1.call-update) | async-done | bytes 1048592 | tf_op jit(solution)/shard_map/psum | solution.py:65
  125.0 11.7 cholesky.374
  136.7 9.8 custom-call.31
  149.2 11.7 cholesky.393
  160.9 10.3 custom-call.32
  172.8 11.7 cholesky.414
  185.2 9.8 custom-call.33
  196.5 11.7 cholesky.431
  212.5 8.0 while.6
  220.6 39.3 %custom-call.34 = f32[4,128,128]{1,2,0:T(8,128)S(1)} custom-call(f32[4,128,128]{2,1,0:T(8,128)S(1)} %get-tuple-element.25), custom_call_target="InvertDiagBlocksLowerTriangular" | custom-call | tf_op jit(solution)/shard_map/jit(_solve_triangular)/triangular_solve | solution.py:67
  284.2 6.2 collective-permute-done
  291.5 4.7 multiply_add_fusion.2
  298.3 58.0 %all-reduce.10.cloned.1.call-done = f32[512,128]{0,1:T(8,128)} async-done(((f32[512,128]{0,1:T(8,128)}), f32[512,128]{0,1:T(8,128)}) %all-reduce.10.cloned.1.call-update) | async-done | bytes 262160 | tf_op jit(solution)/shard_map/psum | solution.py:70
  359.8 19.6 %psum.86 = f32[128]{0:T(128)S(1)} all-reduce(f32[128]{0:T(128)S(1)} %get-tuple-element.195), channel_id=1, replica_groups=mesh['grid'=8,'band'=4] {'grid'}, use_global_device_ids=true, to_apply=%region_11.14 | all-reduce | flops 128 | bytes 1024 | tf_op jit(solution)/shard_map/psum | solution.py:76
  379.7 17.1 %psum.87 = f32[128]{0:T(128)S(1)} all-reduce(f32[128]{0:T(128)S(1)} %multiply_reduce_fusion.4), channel_id=1, replica_groups=mesh['grid'=8,'band'=4] {'grid'}, use_global_device_ids=true, to_apply=%region_13.16 | all-reduce | flops 128 | bytes 1024 | tf_op jit(solution)/shard_map/psum | solution.py:78
  399.9 21.3 %all-gather.8.cloned.1.call-done = f32[4,4,16,16,128]{4,3,2,1,0:T(8,128)} async-done(((f32[1,4,16,16,128]{4,3,2,1,0:T(8,128)}), f32[4,4,16,16,128]{4,3,2,1,0:T(8,128)}) %all-gather.8.cloned.1.call-update) | async-done | bytes 2097168 | tf_op jit(solution)/shard_map/all_gather | solution.py:63
  430.5 78.0 %all-reduce.12.cloned.1.call-done = f32[512,512]{0,1:T(8,128)} async-done(((f32[512,512]{0,1:T(8,128)}), f32[512,512]{0,1:T(8,128)}) %all-reduce.12.cloned.1.call-update) | async-done | bytes 1048592 | tf_op jit(solution)/shard_map/psum | solution.py:65
  513.6 11.7 cholesky.446
  525.4 9.8 custom-call.35
  537.8 11.7 cholesky.465
  550.8 9.9 custom-call.36
  563.3 11.7 cholesky.486
  576.4 9.8 custom-call.37
  588.5 11.7 cholesky.503
  606.8 12.0 while.7
  619.5 40.1 %custom-call.38 = f32[4,128,128]{1,2,0:T(8,128)S(1)} custom-call(f32[4,128,128]{2,1,0:T(8,128)} %copy-done.48), custom_call_target="InvertDiagBlocksLowerTriangular" | custom-call | tf_op jit(solution)/shard_map/jit(_solve_triangular)/triangular_solve | solution.py:67
  685.2 14.3 %collective-permute-done.2 = f32[4,16,16,128]{3,2,1,0:T(8,128)} collective-permute-done((f32[4,16,16,128]{3,2,1,0:T(8,128)S(1)}, f32[4,16,16,128]{3,2,1,0:T(8,128)}, u32[]{:S(2)}, u32[]{:S(2)}) %collective-permute-start.2) | collective-permute-done | bytes 524320 | tf_op jit(solution)/shard_map/ppermute | solution.py:22
  699.6 4.6 multiply_add_fusion.1
  706.3 51.0 %all-reduce.14.cloned.1.call-done = f32[512,128]{0,1:T(8,128)} async-done(((f32[512,128]{0,1:T(8,128)}), f32[512,128]{0,1:T(8,128)}) %all-reduce.14.cloned.1.call-update) | async-done | bytes 262160 | tf_op jit(solution)/shard_map/psum | solution.py:70
  760.9 19.6 %psum.90 = f32[128]{0:T(128)S(1)} all-reduce(f32[128]{0:T(128)S(1)} %get-tuple-element.199), channel_id=1, replica_groups=mesh['grid'=8,'band'=4] {'grid'}, use_global_device_ids=true, to_apply=%region_17.20 | all-reduce | flops 128 | bytes 1024 | tf_op jit(solution)/shard_map/psum | solution.py:76
  780.7 17.1 %psum.91 = f32[128]{0:T(128)S(1)} all-reduce(f32[128]{0:T(128)S(1)} %multiply_reduce_fusion.2), channel_id=1, replica_groups=mesh['grid'=8,'band'=4] {'grid'}, use_global_device_ids=true, to_apply=%region_19.22 | all-reduce | flops 128 | bytes 1024 | tf_op jit(solution)/shard_map/psum | solution.py:78
  801.4 21.3 %all-gather.10.cloned.1.call-done = f32[4,4,16,16,128]{4,3,2,1,0:T(8,128)} async-done(((f32[1,4,16,16,128]{4,3,2,1,0:T(8,128)}), f32[4,4,16,16,128]{4,3,2,1,0:T(8,128)}) %all-gather.10.cloned.1.call-update) | async-done | bytes 2097168 | tf_op jit(solution)/shard_map/all_gather | solution.py:63
  831.8 78.2 %all-reduce.16.cloned.1.call-done = f32[512,512]{0,1:T(8,128)} async-done(((f32[512,512]{0,1:T(8,128)}), f32[512,512]{0,1:T(8,128)}) %all-reduce.16.cloned.1.call-update) | async-done | bytes 1048592 | tf_op jit(solution)/shard_map/psum | solution.py:65
  915.1 11.7 cholesky.518
  927.0 9.8 custom-call.39
  939.3 11.7 cholesky.537
  952.4 10.0 custom-call.40
  964.9 11.7 cholesky.558
  978.0 9.8 custom-call.41
  990.1 11.7 cholesky.575
  1008.6 12.0 while.8
  1021.3 40.1 %custom-call.42 = f32[4,128,128]{1,2,0:T(8,128)S(1)} custom-call(f32[4,128,128]{2,1,0:T(8,128)} %copy-done.47), custom_call_target="InvertDiagBlocksLowerTriangular" | custom-call | tf_op jit(solution)/shard_map/jit(_solve_triangular)/triangular_solve | solution.py:67
  1086.6 14.7 %collective-permute-done.4 = f32[4,16,16,128]{3,2,1,0:T(8,128)} collective-permute-done((f32[4,16,16,128]{3,2,1,0:T(8,128)S(1)}, f32[4,16,16,128]{3,2,1,0:T(8,128)}, u32[]{:S(2)}, u32[]{:S(2)}) %collective-permute-start.4) | collective-permute-done | bytes 524320 | tf_op jit(solution)/shard_map/ppermute | solution.py:22
  1101.4 4.6 multiply_add_fusion
  1108.1 51.1 %all-reduce.18.cloned.1.call-done = f32[512,128]{0,1:T(8,128)} async-done(((f32[512,128]{0,1:T(8,128)}), f32[512,128]{0,1:T(8,128)}) %all-reduce.18.cloned.1.call-update) | async-done | bytes 262160 | tf_op jit(solution)/shard_map/psum | solution.py:70
  1162.7 19.6 %psum.94 = f32[128]{0:T(128)S(1)} all-reduce(f32[128]{0:T(128)S(1)} %get-tuple-element.203), channel_id=1, replica_groups=mesh['grid'=8,'band'=4] {'grid'}, use_global_device_ids=true, to_apply=%region_23.26 | all-reduce | flops 128 | bytes 1024 | tf_op jit(solution)/shard_map/psum | solution.py:76
  1182.5 17.1 %psum.95 = f32[128]{0:T(128)S(1)} all-reduce(f32[128]{0:T(128)S(1)} %multiply_reduce_fusion), channel_id=1, replica_groups=mesh['grid'=8,'band'=4] {'grid'}, use_global_device_ids=true, to_apply=%region_25.28 | all-reduce | flops 128 | bytes 1024 | tf_op jit(solution)/shard_map/psum | solution.py:78
  (338 shorter events, 213.5 us)
Async XLA Ops:
  7.2 27.7 %all-gather.12.cloned.1.call-start = ((), (), s32[]{:S(2)}) async-start(), calls=%async_computation.9 | async-start | bytes 2621440 | tf_op jit(solution)/shard_map/all_gather | solution.py:63
  7.9 114.2 %all-reduce.8.cloned.1.call-start = ((), (), s32[]{:S(2)}) async-start(), calls=%async_computation | async-start | bytes 2097152 | tf_op jit(solution)/shard_map/psum | solution.py:65
  43.6 236.5 %all-gather.6.cloned.1.call-start = ((), (), s32[]{:S(2)}) async-start(), calls=%async_computation.1 | async-start | bytes 2621440 | tf_op jit(solution)/shard_map/all_gather | solution.py:55
  44.4 311.9 %all-reduce.10.cloned.1.call-start = ((), (), s32[]{:S(2)}) async-start(), calls=%async_computation.2 | async-start | bytes 524288 | tf_op jit(solution)/shard_map/psum | solution.py:70
  44.8 217.1 %copy-start.1 = (f32[512,512]{1,0:T(8,128)}, f32[512,512]{1,0:T(8,128)S(1)}, u32[]{:S(2)}) copy-start(f32[512,512]{1,0:T(8,128)S(1)} %fusion.24) | copy-start | bytes 3145732
  265.5 24.9 %collective-permute-start = (f32[4,16,16,128]{3,2,1,0:T(8,128)S(1)}, f32[4,16,16,128]{3,2,1,0:T(8,128)S(1)}, u32[]{:S(2)}, u32[]{:S(2)}) collective-permute-start(f32[4,16,16,128]{3,2,1,0:T(8,128)S(1)} %bitcast.260), channel_id=1, source_target_pairs={{4,0},{8,4},{12,8},{16,12},{20,16},{24,20},{28,24},{0,28},{5,1},{9... | collective-permute-start | bytes 1572872 | tf_op jit(solution)/shard_map/ppermute | solution.py:22
  268.5 21.9 %collective-permute-start.1 = (f32[4,16,16,128]{3,2,1,0:T(8,128)S(1)}, f32[4,16,16,128]{3,2,1,0:T(8,128)S(1)}, u32[]{:S(2)}, u32[]{:S(2)}) collective-permute-start(f32[4,16,16,128]{3,2,1,0:T(8,128)S(1)} %bitcast.261), channel_id=1, source_target_pairs={{0,4},{4,8},{8,12},{12,16},{16,20},{20,24},{24,28},{28,0},{1,5},{5... | collective-permute-start | bytes 1572872 | tf_op jit(solution)/shard_map/ppermute | solution.py:19
  283.7 137.5 %all-gather.8.cloned.1.call-start = ((), (), s32[]{:S(2)}) async-start(), calls=%async_computation.3 | async-start | bytes 2621440 | tf_op jit(solution)/shard_map/all_gather | solution.py:63
  284.0 7.5 copy-start.30
  284.0 7.4 copy-start.31
  284.0 7.4 copy-start.32
  284.0 7.4 copy-start.33
  284.0 7.4 copy-start.34
  284.0 7.4 copy-start.35
  284.1 7.4 copy-start.40
  284.1 7.4 copy-start.41
  284.1 7.4 copy-start.44
  291.5 64.8 %copy-start = (f32[4,16,16,512]{3,2,1,0:T(8,128)S(1)}, f32[4,16,16,512]{3,2,1,0:T(8,128)}, u32[]{:S(2)}) copy-start(f32[4,16,16,512]{3,2,1,0:T(8,128)} %all-gather.6.cloned.1.call-done) | copy-start | bytes 6291460
  399.9 108.6 %all-reduce.12.cloned.1.call-start = ((), (), s32[]{:S(2)}) async-start(), calls=%async_computation.4 | async-start | bytes 2097152 | tf_op jit(solution)/shard_map/psum | solution.py:65
  430.1 327.3 %all-reduce.14.cloned.1.call-start = ((), (), s32[]{:S(2)}) async-start(), calls=%async_computation.5 | async-start | bytes 524288 | tf_op jit(solution)/shard_map/psum | solution.py:70
  563.3 96.4 %copy-start.2 = (f32[512,512]{1,0:T(8,128)S(1)}, f32[512,512]{1,0:T(8,128)}, u32[]{:S(2)}) copy-start(f32[512,512]{1,0:T(8,128)} %copy-done.1) | copy-start | bytes 3145732
  673.6 26.0 %collective-permute-start.2 = (f32[4,16,16,128]{3,2,1,0:T(8,128)S(1)}, f32[4,16,16,128]{3,2,1,0:T(8,128)}, u32[]{:S(2)}, u32[]{:S(2)}) collective-permute-start(f32[4,16,16,128]{3,2,1,0:T(8,128)S(1)} %bitcast.228), channel_id=1, source_target_pairs={{4,0},{8,4},{12,8},{16,12},{20,16},{24,20},{28,24},{0,28},{5,1},{9... | collective-permute-start | bytes 1572872 | tf_op jit(solution)/shard_map/ppermute | solution.py:22
  676.5 23.1 %collective-permute-start.3 = (f32[4,16,16,128]{3,2,1,0:T(8,128)S(1)}, f32[4,16,16,128]{3,2,1,0:T(8,128)}, u32[]{:S(2)}, u32[]{:S(2)}) collective-permute-start(f32[4,16,16,128]{3,2,1,0:T(8,128)S(1)} %bitcast.229), channel_id=1, source_target_pairs={{0,4},{4,8},{8,12},{12,16},{16,20},{20,24},{24,28},{28,0},{1,5},{5... | collective-permute-start | bytes 1572872 | tf_op jit(solution)/shard_map/ppermute | solution.py:19
  684.5 138.3 %all-gather.10.cloned.1.call-start = ((), (), s32[]{:S(2)}) async-start(), calls=%async_computation.6 | async-start | bytes 2621440 | tf_op jit(solution)/shard_map/all_gather | solution.py:63
  685.0 14.6 %copy-start.18 = (f32[4,16,15,128]{3,2,1,0:T(8,128)S(1)}, f32[4,16,15,128]{3,2,1,0:T(8,128)}, u32[]{:S(2)}) copy-start(f32[4,16,15,128]{3,2,1,0:T(8,128)} %get-tuple-element.111) | copy-start | bytes 1474564
  685.0 14.6 %copy-start.19 = (f32[4,16,15,128]{3,2,1,0:T(8,128)S(1)}, f32[4,16,15,128]{3,2,1,0:T(8,128)}, u32[]{:S(2)}) copy-start(f32[4,16,15,128]{3,2,1,0:T(8,128)} %get-tuple-element.112) | copy-start | bytes 1474564
  685.0 14.6 %copy-start.20 = (f32[4,16,14,128]{3,2,1,0:T(8,128)S(1)}, f32[4,16,14,128]{3,2,1,0:T(8,128)}, u32[]{:S(2)}) copy-start(f32[4,16,14,128]{3,2,1,0:T(8,128)} %get-tuple-element.115) | copy-start | bytes 1376260
  685.0 14.6 %copy-start.21 = (f32[4,16,14,128]{3,2,1,0:T(8,128)S(1)}, f32[4,16,14,128]{3,2,1,0:T(8,128)}, u32[]{:S(2)}) copy-start(f32[4,16,14,128]{3,2,1,0:T(8,128)} %get-tuple-element.116) | copy-start | bytes 1376260
  685.0 14.6 %copy-start.22 = (f32[4,16,13,128]{3,2,1,0:T(8,128)S(1)}, f32[4,16,13,128]{3,2,1,0:T(8,128)}, u32[]{:S(2)}) copy-start(f32[4,16,13,128]{3,2,1,0:T(8,128)} %get-tuple-element.119) | copy-start | bytes 1277956
  685.0 14.6 %copy-start.23 = (f32[4,16,13,128]{3,2,1,0:T(8,128)S(1)}, f32[4,16,13,128]{3,2,1,0:T(8,128)}, u32[]{:S(2)}) copy-start(f32[4,16,13,128]{3,2,1,0:T(8,128)} %get-tuple-element.120) | copy-start | bytes 1277956
  685.0 14.6 %copy-start.36 = (f32[4,14,16,128]{3,2,1,0:T(8,128)S(1)}, f32[4,14,16,128]{3,2,1,0:T(8,128)}, u32[]{:S(2)}) copy-start(f32[4,14,16,128]{3,2,1,0:T(8,128)} %get-tuple-element.99) | copy-start | bytes 1376260
  685.0 14.6 %copy-start.37 = (f32[4,14,16,128]{3,2,1,0:T(8,128)S(1)}, f32[4,14,16,128]{3,2,1,0:T(8,128)}, u32[]{:S(2)}) copy-start(f32[4,14,16,128]{3,2,1,0:T(8,128)} %get-tuple-element.100) | copy-start | bytes 1376260
  685.0 14.6 %copy-start.45 = (f32[4,16,16]{2,1,0:T(8,128)S(1)}, f32[4,16,16]{2,1,0:T(8,128)}, u32[]{:S(2)}) copy-start(f32[4,16,16]{2,1,0:T(8,128)} %param.8) | copy-start | bytes 12292
  801.4 108.7 %all-reduce.16.cloned.1.call-start = ((), (), s32[]{:S(2)}) async-start(), calls=%async_computation.7 | async-start | bytes 2097152 | tf_op jit(solution)/shard_map/psum | solution.py:65
  831.6 327.6 %all-reduce.18.cloned.1.call-start = ((), (), s32[]{:S(2)}) async-start(), calls=%async_computation.8 | async-start | bytes 524288 | tf_op jit(solution)/shard_map/psum | solution.py:70
  964.9 96.6 %copy-start.3 = (f32[512,512]{1,0:T(8,128)S(1)}, f32[512,512]{1,0:T(8,128)}, u32[]{:S(2)}) copy-start(f32[512,512]{1,0:T(8,128)} %copy-done.1) | copy-start | bytes 3145732
  1075.4 26.0 %collective-permute-start.4 = (f32[4,16,16,128]{3,2,1,0:T(8,128)S(1)}, f32[4,16,16,128]{3,2,1,0:T(8,128)}, u32[]{:S(2)}, u32[]{:S(2)}) collective-permute-start(f32[4,16,16,128]{3,2,1,0:T(8,128)S(1)} %bitcast.247), channel_id=1, source_target_pairs={{4,0},{8,4},{12,8},{16,12},{20,16},{24,20},{28,24},{0,28},{5,1},{9... | collective-permute-start | bytes 1572872 | tf_op jit(solution)/shard_map/ppermute | solution.py:22
  1078.3 23.1 %collective-permute-start.5 = (f32[4,16,16,128]{3,2,1,0:T(8,128)S(1)}, f32[4,16,16,128]{3,2,1,0:T(8,128)}, u32[]{:S(2)}, u32[]{:S(2)}) collective-permute-start(f32[4,16,16,128]{3,2,1,0:T(8,128)S(1)} %bitcast.248), channel_id=1, source_target_pairs={{0,4},{4,8},{8,12},{12,16},{16,20},{20,24},{24,28},{28,0},{1,5},{5... | collective-permute-start | bytes 1572872 | tf_op jit(solution)/shard_map/ppermute | solution.py:19
  1086.4 15.0 %copy-start.24 = (f32[4,16,15,128]{3,2,1,0:T(8,128)S(1)}, f32[4,16,15,128]{3,2,1,0:T(8,128)}, u32[]{:S(2)}) copy-start(f32[4,16,15,128]{3,2,1,0:T(8,128)} %get-tuple-element.79) | copy-start | bytes 1474564
  1086.4 15.0 %copy-start.25 = (f32[4,16,15,128]{3,2,1,0:T(8,128)S(1)}, f32[4,16,15,128]{3,2,1,0:T(8,128)}, u32[]{:S(2)}) copy-start(f32[4,16,15,128]{3,2,1,0:T(8,128)} %get-tuple-element.80) | copy-start | bytes 1474564
  1086.4 15.0 %copy-start.26 = (f32[4,16,14,128]{3,2,1,0:T(8,128)S(1)}, f32[4,16,14,128]{3,2,1,0:T(8,128)}, u32[]{:S(2)}) copy-start(f32[4,16,14,128]{3,2,1,0:T(8,128)} %get-tuple-element.83) | copy-start | bytes 1376260
  1086.4 15.0 %copy-start.27 = (f32[4,16,14,128]{3,2,1,0:T(8,128)S(1)}, f32[4,16,14,128]{3,2,1,0:T(8,128)}, u32[]{:S(2)}) copy-start(f32[4,16,14,128]{3,2,1,0:T(8,128)} %get-tuple-element.84) | copy-start | bytes 1376260
  1086.4 15.0 %copy-start.28 = (f32[4,16,13,128]{3,2,1,0:T(8,128)S(1)}, f32[4,16,13,128]{3,2,1,0:T(8,128)}, u32[]{:S(2)}) copy-start(f32[4,16,13,128]{3,2,1,0:T(8,128)} %get-tuple-element.87) | copy-start | bytes 1277956
  1086.4 15.0 %copy-start.29 = (f32[4,16,13,128]{3,2,1,0:T(8,128)S(1)}, f32[4,16,13,128]{3,2,1,0:T(8,128)}, u32[]{:S(2)}) copy-start(f32[4,16,13,128]{3,2,1,0:T(8,128)} %get-tuple-element.88) | copy-start | bytes 1277956
  1086.4 15.0 %copy-start.38 = (f32[4,14,16,128]{3,2,1,0:T(8,128)S(1)}, f32[4,14,16,128]{3,2,1,0:T(8,128)}, u32[]{:S(2)}) copy-start(f32[4,14,16,128]{3,2,1,0:T(8,128)} %get-tuple-element.67) | copy-start | bytes 1376260
  1086.5 15.0 %copy-start.39 = (f32[4,14,16,128]{3,2,1,0:T(8,128)S(1)}, f32[4,14,16,128]{3,2,1,0:T(8,128)}, u32[]{:S(2)}) copy-start(f32[4,14,16,128]{3,2,1,0:T(8,128)} %get-tuple-element.68) | copy-start | bytes 1376260
  1086.5 15.0 %copy-start.46 = (f32[4,16,16]{2,1,0:T(8,128)S(1)}, f32[4,16,16]{2,1,0:T(8,128)}, u32[]{:S(2)}) copy-start(f32[4,16,16]{2,1,0:T(8,128)} %param.8) | copy-start | bytes 12292
  1162.7 38.2 %copy-start.49 = (f32[1,128]{1,0:T(1,128)S(1)}, f32[1,128]{1,0:T(1,128)}, u32[]{:S(2)}) copy-start(f32[1,128]{1,0:T(1,128)} %get-tuple-element.189) | copy-start | bytes 1540
  (18 other events, 30.2 us)
Sparse Core Ops, SparseCore 0:
  9.5 25.2 all-gather.11
  43.8 78.2 all-reduce.7
  123.6 22.4 all-gather.5
  283.9 72.4 all-reduce.9
  400.0 21.2 all-gather.7
  430.2 78.2 all-reduce.11
  684.6 72.6 all-reduce.13
  801.5 21.2 all-gather.9
  831.7 78.2 all-reduce.15
  1086.5 72.6 all-reduce.17
